TPU v7x, 32 devices: a 4x4x1 block of a 4x4x8 slice. The times are simulated.
32 devices in a mesh: member: 1 (over z), ty: 4 (over y), tx: 4 (over x), panel: 2 (over core).
Axes of the slice: x: 4, y: 4, z: 1, core: 2. Of those that a mesh axis runs over, the one named last changes fastest.
The devices are a block of a 4x4x8 slice.
Arguments:
- tracer: float32 [6, 720, 720], P(('member', 'panel'), 'tx', 'ty')
- wind_a: float32 [6, 720, 720], P('panel', 'tx', 'ty')
- wind_b: float32 [6, 720, 720], P('panel', 'tx', 'ty')
- wind_scale: float32 [64], replicated
Outputs:
- output: float32 [6, 720, 720], P(('member', 'panel'), 'tx', 'ty')
All inputs are finite; a program needn't handle non-finite values.
Results may differ from a plain program's by a relative error of at most 0.001.
Values sent between devices are 32-bit elements.
A program may use at most 768 MiB of HBM per device.

v0:
```python
import math
import jax
import jax.numpy as jnp
from jax import lax
from jax.sharding import PartitionSpec as P

C_SPEED = 2.5
CFL_STEP = 0.12
EDGE_TABLE = (
    ((3, 1, 0), (1, 0, 0), (5, 3, 0), (4, 2, 0)),
    ((0, 1, 0), (2, 0, 0), (5, 1, 1), (4, 1, 0)),
    ((1, 1, 0), (3, 0, 0), (5, 2, 1), (4, 3, 1)),
    ((2, 1, 0), (0, 0, 0), (5, 0, 0), (4, 0, 1)),
    ((3, 3, 1), (1, 3, 0), (0, 3, 0), (2, 3, 1)),
    ((3, 2, 0), (1, 2, 1), (2, 2, 1), (0, 2, 0)),
)


def edge_sign(side_id, edge_id):
    out_sign = 1.0 if edge_id in (1, 3) else -1.0
    return out_sign if side_id in (0, 2) else -out_sign


def out_strips(field_a, field_b):
    return (field_a[:, 0:2, :],
            jnp.flip(field_a[:, -2:, :], axis=1),
            jnp.swapaxes(field_b[:, :, 0:2], 1, 2),
            jnp.swapaxes(jnp.flip(field_b[:, :, -2:], axis=2), 1, 2))


def to_blocks(ghosts):
    return (jnp.flip(ghosts[0], axis=1), ghosts[1],
            jnp.swapaxes(jnp.flip(ghosts[2], axis=1), 1, 2), jnp.swapaxes(ghosts[3], 1, 2))


def extend_field(field_now, blocks):
    return (jnp.concatenate([blocks[0], field_now, blocks[1]], axis=1),
            jnp.concatenate([blocks[2], field_now, blocks[3]], axis=2))


def wind_faces(blocks, wind_a, wind_b):
    ext_a = jnp.concatenate([blocks[0][:, 1:2, :], wind_a, blocks[1][:, 0:1, :]], axis=1)
    ext_b = jnp.concatenate([blocks[2][:, :, 1:2], wind_b, blocks[3][:, :, 0:1]], axis=2)
    return 0.5 * (ext_a[:, :-1, :] + ext_a[:, 1:, :]), 0.5 * (ext_b[:, :, :-1] + ext_b[:, :, 1:])


def face_flux_div(ext_arr, wind_face, step_scale, axis_id):
    face_count = ext_arr.shape[axis_id] - 3
    far_left = lax.slice_in_dim(ext_arr, 0, face_count, axis=axis_id)
    near_left = lax.slice_in_dim(ext_arr, 1, face_count + 1, axis=axis_id)
    near_right = lax.slice_in_dim(ext_arr, 2, face_count + 2, axis=axis_id)
    far_right = lax.slice_in_dim(ext_arr, 3, face_count + 3, axis=axis_id)
    face_val = (7.0 * (near_left + near_right) - (far_left + far_right)) / 12.0
    face_flux = step_scale * wind_face * face_val - (0.5 * C_SPEED) * (near_right - near_left)
    return (lax.slice_in_dim(face_flux, 1, face_count, axis=axis_id)
            - lax.slice_in_dim(face_flux, 0, face_count - 1, axis=axis_id))


def tendency(ext_a, ext_b, face_a, face_b, step_scale, inv_area):
    div_total = face_flux_div(ext_a, face_a, step_scale, 1) + face_flux_div(ext_b, face_b, step_scale, 2)
    return -div_total * inv_area


def inverse_area(row_ids, col_ids, cells):
    dalpha = 0.5 * math.pi / cells
    tan_a = jnp.tan((row_ids.astype(jnp.float32) + 0.5) * dalpha - 0.25 * math.pi)[:, None]
    tan_b = jnp.tan((col_ids.astype(jnp.float32) + 0.5) * dalpha - 0.25 * math.pi)[None, :]
    r_sq = 1.0 + tan_a * tan_a + tan_b * tan_b
    sqrt_g = (1.0 + tan_a * tan_a) * (1.0 + tan_b * tan_b) / (r_sq * jnp.sqrt(r_sq))
    return 1.0 / (dalpha * sqrt_g)


def solution(mesh):
    tile_count = mesh.shape['tx']
    panel_count = mesh.shape['panel']
    local_panels = 6 // panel_count
    group_axes = ('ty', 'tx', 'panel')
    field_spec = P(('member', 'panel'), 'tx', 'ty')
    wind_spec = P('panel', 'tx', 'ty')
    shift_up = [(idx_src, idx_src + 1) for idx_src in range(tile_count - 1)]
    shift_down = [(idx_src + 1, idx_src) for idx_src in range(tile_count - 1)]

    def device_id(panel_dev, tile_pos):
        return (tile_pos[1] * tile_count + tile_pos[0]) * panel_count + panel_dev

    def edge_tile(side_id, along_idx):
        last_idx = tile_count - 1
        return ((0, along_idx), (last_idx, along_idx), (along_idx, 0), (along_idx, last_idx))[side_id]

    cross_plan = []
    for panel_id in range(6):
        for side_id in range(4):
            src_panel, edge_id, flipped = EDGE_TABLE[panel_id][side_id]
            perm_pairs = []
            for along_idx in range(tile_count):
                src_along = tile_count - 1 - along_idx if flipped else along_idx
                perm_pairs.append((device_id(src_panel // local_panels, edge_tile(edge_id, src_along)),
                                   device_id(panel_id // local_panels, edge_tile(side_id, along_idx))))
            cross_plan.append((panel_id % local_panels, side_id, src_panel % local_panels, edge_id, flipped, perm_pairs))

    def fill_halo(field_a, field_b, signed):
        strips = out_strips(field_a, field_b)
        received = {}
        for slot_id, side_id, src_slot, edge_id, flipped, perm_pairs in cross_plan:
            one_strip = strips[edge_id][src_slot]
            if flipped:
                one_strip = jnp.flip(one_strip, axis=1)
            if signed:
                one_strip = edge_sign(side_id, edge_id) * one_strip
            moved_strip = lax.ppermute(one_strip, group_axes, perm_pairs)
            received[(side_id, slot_id)] = received.get((side_id, slot_id), 0.0) + moved_strip
        cross_blks = to_blocks([jnp.stack([received[(side_id, slot_id)] for slot_id in range(local_panels)])
                                for side_id in range(4)])
        own_blks = (lax.ppermute(field_a[:, -2:, :], 'tx', shift_up),
                    lax.ppermute(field_a[:, 0:2, :], 'tx', shift_down),
                    lax.ppermute(field_b[:, :, -2:], 'ty', shift_up),
                    lax.ppermute(field_b[:, :, 0:2], 'ty', shift_down))
        return tuple(own_blk + cross_blk for own_blk, cross_blk in zip(own_blks, cross_blks))

    def local_run(tracer, wind_a, wind_b, wind_scale):
        tile_rows = tracer.shape[1]
        tile_cols = tracer.shape[2]
        cells = tile_rows * tile_count
        time_step = CFL_STEP * (0.5 * math.pi / cells)
        row_ids = lax.axis_index('tx') * tile_rows + jnp.arange(tile_rows)
        col_ids = lax.axis_index('ty') * tile_cols + jnp.arange(tile_cols)
        inv_area = inverse_area(row_ids, col_ids, cells)
        face_a, face_b = wind_faces(fill_halo(wind_a, wind_b, True), wind_a, wind_b)

        def tend_of(tracer_now, step_scale):
            ext_a, ext_b = extend_field(tracer_now, fill_halo(tracer_now, tracer_now, False))
            return tendency(ext_a, ext_b, face_a, face_b, step_scale, inv_area)

        def one_step(step_id, tracer_now):
            step_scale = wind_scale[step_id]
            stage_one = tracer_now + time_step * tend_of(tracer_now, step_scale)
            stage_two = stage_one + time_step * tend_of(stage_one, step_scale)
            return 0.5 * (tracer_now + stage_two)

        return lax.fori_loop(0, wind_scale.shape[0], one_step, tracer)

    return jax.shard_map(local_run, mesh=mesh, in_specs=(field_spec, wind_spec, wind_spec, P()),
                         out_specs=field_spec, check_vma=False)
```

profile of v0, /device:TPU:97, one launch (start us, length us, event | category | flops | bytes accessed | tf_op | source)
XLA Modules:
  0.0 10563.0 jit_solution(15639115109794140386)
XLA Ops:
  61.5 10500.6 %while.14 = (s32[]{:T(128)}, f32[3,180,180]{2,1,0:T(8,128)S(1)}, f32[64]{0:T(128)S(1)}, f32[3,181,180]{2,1,0:T(8,128)S(1)}, f32[3,180,181]{2,1,0:T(8,128)S(1)}, ...) while((s32[]{:T(128)}, f32[3,180,180]{2,1,0:T(8,128)S(1)}, ...), condition=%wide.region_1.2_spmd.clone, body=%wide.region_0.1_spmd.clone.sunk | while | flops 7257602 | bytes 12017273 | solution.py:140
  222.2 13.9 collective-permute-start.5
  386.4 13.9 collective-permute-start.5
  550.7 13.9 collective-permute-start.5
  714.9 13.9 collective-permute-start.5
  879.1 13.9 collective-permute-start.5
  1864.5 13.9 collective-permute-start.5
  2028.8 13.9 collective-permute-start.5
  2849.9 13.9 collective-permute-start.5
  3014.2 13.9 collective-permute-start.5
  3835.3 13.9 collective-permute-start.5
  3999.6 13.9 collective-permute-start.5
  4985.0 13.9 collective-permute-start.5
  5149.2 13.9 collective-permute-start.5
  5970.4 13.9 collective-permute-start.5
  6134.6 13.9 collective-permute-start.5
  6955.8 13.9 collective-permute-start.5
  7120.0 13.9 collective-permute-start.5
  8105.5 13.9 collective-permute-start.5
  8269.7 13.9 collective-permute-start.5
  9090.9 13.9 collective-permute-start.5
  9255.1 13.9 collective-permute-start.5
  10076.3 13.9 collective-permute-start.5
  10240.5 13.9 collective-permute-start.5
  (15587 shorter events, 10157.8 us)
Async XLA Ops:
  126.8 83.6 collective-permute-start.35
  292.8 81.8 collective-permute-start.35
  785.5 81.8 collective-permute-start.35
  949.7 81.8 collective-permute-start.35
  1114.0 81.8 collective-permute-start.35
  1278.2 81.8 collective-permute-start.35
  1770.9 81.8 collective-permute-start.35
  1935.1 81.8 collective-permute-start.35
  2099.4 81.8 collective-permute-start.35
  2263.6 81.8 collective-permute-start.35
  2756.3 81.8 collective-permute-start.35
  2920.5 81.8 collective-permute-start.35
  3084.8 81.8 collective-permute-start.35
  3249.0 81.8 collective-permute-start.35
  3413.2 81.8 collective-permute-start.35
  3906.0 81.8 collective-permute-start.35
  4070.2 81.8 collective-permute-start.35
  4234.4 81.8 collective-permute-start.35
  4398.7 81.8 collective-permute-start.35
  4891.4 81.8 collective-permute-start.35
  5055.6 81.8 collective-permute-start.35
  5219.8 81.8 collective-permute-start.35
  5384.1 81.8 collective-permute-start.35
  5876.8 81.8 collective-permute-start.35
  (4489 other events, 49166.6 us)
where the time goes:
time: 10700 us; the launch traced here: 10600 us
  starting transfers between devices  6240 us (58%)
  waiting for transfers between devices  2070 us (19%)
  local copies, waits for them, and re-layouts  1210 us (11%)
  other arithmetic  952 us (9%)
    ppermute x3096, starting transfers between devices, fill_halo(): moved_strip = lax.ppermute(one_strip, group_axes, perm_pairs)  5000 us
    ppermute x3096, waiting for transfers between devices, fill_halo(): moved_strip = lax.ppermute(one_strip, group_axes, perm_pairs)  2070 us
    ppermute x129, starting transfers between devices, fill_halo(): lax.ppermute(field_a[:, -2:, :], 'tx', shift_up)  518 us
    another operation x1742, other arithmetic, fill_halo(): jnp.stack([received[side_id, slot_id] for slot_id in range(local_panels)])  411 us
    ppermute x129, starting transfers between devices, fill_halo(): lax.ppermute(field_b[:, :, -2:], 'ty', shift_up)  387 us
    rev x448, local copies, waits for them, and re-layouts, fill_halo(): one_strip = jnp.flip(one_strip, axis=1)  380 us
    sub x256, other arithmetic, face_flux_div(): step_scale * wind_face * face_val - 0.5 * C_SPEED * (near_right - near_left)  311 us
    while x2944, local copies, waits for them, and re-layouts  252 us

commit v1 on v0

v1 whole, which is shorter than its diff:
```python
import functools
import math
import jax
import jax.numpy as jnp
from jax import lax
from jax.experimental import pallas as pl
from jax.experimental.pallas import tpu as pltpu
from jax.sharding import PartitionSpec as P

C_SPEED = 2.5
CFL_STEP = 0.12
EDGES = ('310,100,530,420', '010,200,511,410', '110,300,521,431', '210,000,500,401', '331,130,030,231', '320,121,221,020')
EDGE_TABLE = [[[int(digit) for digit in side] for side in panel.split(',')] for panel in EDGES]

LANES = 128
NV = 16
NW = 4
OFF = 38
HALO = 32
STEPS_PER_ROUND = 8
NIBBLE = 4
SUBS = 8
HALF = 64
PAIR = range(2)
QUADS = range(4)
ORDERS = {'a': '210', 'b': '201', 'c': '120', 'd': '102'}
ORDER_OF = 'abbbaaaacccccccc' + 'bacdbacdbacdaacd'
F32 = jnp.float32
I32 = jnp.int32
MESH_ID = pl.DeviceIdType.MESH


def lane_id():
    return lax.broadcasted_iota(I32, (SUBS, LANES), 1)


def sub_id():
    return lax.broadcasted_iota(I32, (SUBS, LANES), 0)


def lanes_of(val, idx):
    return jnp.take_along_axis(val, idx, axis=1, mode="promise_in_bounds")


def rev8(val):
    return jnp.take_along_axis(val, 7 - sub_id(), axis=0, mode="promise_in_bounds")


def pick(sel, vals):
    if isinstance(sel, int):
        return vals[sel]
    out = vals[-1]
    for i in range(len(vals) - 2, -1, -1):
        out = jnp.where(sel == i, vals[i], out)
    return out


def reg(v):
    return pl.ds(SUBS * v, SUBS)


def at(pos):
    return pl.ds(pos, SUBS)


def nat(t):
    return pl.ds(HALF * (t & 1) + (t >> 1), 8, stride=8)


class Where:
    def __init__(self, tiles, panels_per_dev):
        self.n, self.lp = tiles, panels_per_dev
        self.tx, self.ty, self.pd = lax.axis_index('tx'), lax.axis_index('ty'), lax.axis_index('panel')
        self.ftx, self.fty = self.flip(self.tx), self.flip(self.ty)
        self.edge_x = self.at_edge(self.tx)
        self.edge_y = self.at_edge(self.ty)
        self.vertex = self.edge_x * self.edge_y

    def flip(self, t):
        return lax.div(t, jnp.int32(self.n // 2))

    def at_edge(self, t):
        return jnp.where(t == 0, 1, jnp.where(t == self.n - 1, 1, 0))

    @staticmethod
    def xor(a, b):
        return a + b - 2 * a * b

    def lookup(self, panel, base, bit):
        code = None
        for p in range(6):
            lo, hi = (np * 8 + e * 2 + fl for np, e, fl in (EDGE_TABLE[p][base], EDGE_TABLE[p][base + 1]))
            val = lo + bit * (hi - lo)
            code = val if code is None else jnp.where(panel == p, val, code)
        return code

    def cross(self, slot, base, bit, along, along_half):
        code = self.lookup(self.lp * self.pd + slot, base, bit)
        np_, e, fl = code >> 3, (code >> 1) & 3, code & 1
        al = along + fl * (self.n - 1 - 2 * along)
        alh = self.xor(along_half, fl)
        col, end = e >> 1, e & 1
        far = end * (self.n - 1)
        tx = far + col * (al - far)
        ty = al + col * (far - al)
        hp = end + col * (alh - end)
        kp = alh + col * (end - alh)
        pd = lax.div(np_, jnp.int32(self.lp))
        return (pd, np_ - pd * self.lp, tx, ty, self.xor(hp, self.flip(tx)), self.xor(kp, self.flip(ty)), col)

    def mix(self, flag, a, b):
        return tuple(x + flag * (y - x) for x, y in zip(a, b))

    def face(self, slot, h, k, kind):
        hp, kp = self.xor(h, self.ftx), self.xor(k, self.fty)
        if kind == 0:
            tx = self.tx + 2 * hp - 1
            inner = (self.pd, slot, tx, self.ty, self.xor(1 - hp, self.flip(tx)), k, 0)
            return self.mix((1 - h) * self.edge_x, inner, self.cross(slot, 0, hp, self.ty, kp))
        ty = self.ty + 2 * kp - 1
        inner = (self.pd, slot, self.tx, ty, h, self.xor(1 - kp, self.flip(ty)), 1)
        return self.mix((1 - k) * self.edge_y, inner, self.cross(slot, 2, kp, self.tx, hp))

    def corner(self, slot, h, k):
        hp, kp = self.xor(h, self.ftx), self.xor(k, self.fty)
        tx, ty = self.tx + 2 * hp - 1, self.ty + 2 * kp - 1
        dest = (self.pd, slot, tx, ty, self.xor(1 - hp, self.flip(tx)), self.xor(1 - kp, self.flip(ty)), 0)
        d = self.cross(slot, 2, kp, tx, 1 - hp)
        dest = self.mix((1 - k) * self.edge_y, dest, d[:6] + (1 - d[6],))
        return self.mix((1 - h) * self.edge_x, dest, self.cross(slot, 0, hp, ty, 1 - kp))


def kernel(tiles, steps, size, ws, in_ref, k_in, out, st, xb, fr, fc, fcm, kk, mm, vcoef, vbuf, vcol, vrow, roll_buf, row_buf, nat_buf, turn,
           strip, strip_c, rbuf, rbuf_c, send_sem, recv_sem):
    slots = out.shape[0]
    lane, sub = lane_id(), sub_id()
    lb, half = lane & 63, lane >> 6
    here = Where(tiles, slots)
    rounds = steps // STEPS_PER_ROUND
    vertex = here.vertex == 1

    def loop(count, fn, first=0):
        def body(i, carry):
            fn(i)
            return carry
        lax.fori_loop(first, count, body, 0)

    def plan(slot, qd, kind):
        h, k = qd >> 1, qd & 1
        dest = here.corner(slot, h, k) if kind == 2 else here.face(slot, h, k, kind)
        code = dest[0]
        for i, part in enumerate((dest[1], dest[2], dest[3], 2 * dest[4] + dest[5], dest[6])):
            code = code + (part << (NIBBLE * (i + 1)))
        if kind == 2:
            stays = vertex & (qd == 0)
        else:
            stays = (dest[0] == here.pd) & (dest[2] == here.tx) & (dest[3] == here.ty)
        return code + jnp.where(stays, 1 << (6 * NIBBLE), 0)

    plans = [[[plan(slot, qd, kind) for kind in range(3)] for qd in QUADS] for slot in range(slots)]

    def code_of(slot, qd, kind):
        return pick(slot, [plans[i][qd][kind] for i in range(slots)])

    def to(slot, qd, kind):
        code = code_of(slot, qd, kind)
        pd, slot2, tx, ty, qd2, kind2 = [(code >> (NIBBLE * i)) & ((1 << NIBBLE) - 1) for i in range(6)]
        return {'panel': pd, 'tx': tx, 'ty': ty}, slot2, qd2, kind2, (code >> (6 * NIBBLE)) == 1

    def leaves(slot, qd, kind):
        return (code_of(slot, qd, kind) >> (6 * NIBBLE)) == 0

    def send(field, set_id, slot):
        for qd in QUADS:
            for kind in range(3):
                device, slot2, qd2, kind2, stays = to(slot, qd, kind)
                if kind < 2:
                    src, dst = strip.at[field, slot, qd, kind, pl.ds(SUBS, HALO)], rbuf.at[set_id, slot2, qd2, kind2]
                    sem = recv_sem.at[set_id, slot2, qd2, kind2]
                else:
                    src, dst = strip_c.at[field, slot, qd, kind2], rbuf_c.at[set_id, slot2, qd2]
                    sem = recv_sem.at[set_id, slot2, qd2, 2]

                @pl.when(jnp.logical_not(stays))
                def _():
                    pltpu.make_async_remote_copy(
                        src_ref=src, dst_ref=dst, send_sem=send_sem.at[field, slot, qd, kind], recv_sem=sem,
                        device_id=device, device_id_type=MESH_ID).start()

                if kind < 2 and (qd >> 1, qd & 1)[kind] == 0:
                    @pl.when(stays)
                    def _():
                        for g in QUADS:
                            rbuf[set_id, slot2, qd2, kind2, reg(g), :] = (
                                strip[field, slot, qd, kind, at(8 + SUBS * g), :])

    def wait_all(field, set_id, slot, sent):
        for qd in QUADS:
            for kind in range(3):
                if kind < 2:
                    src, dst = strip.at[field, slot, qd, kind, pl.ds(SUBS, HALO)], rbuf.at[set_id, slot, qd, kind]
                else:
                    src, dst = strip_c.at[field, slot, qd, 0], rbuf_c.at[set_id, slot, qd]

                def wait():
                    copy = pltpu.make_async_remote_copy(
                        src_ref=src, dst_ref=dst, send_sem=send_sem.at[field, slot, qd, kind],
                        recv_sem=recv_sem.at[set_id, slot, qd, kind],
                        device_id={'panel': here.pd, 'tx': here.tx, 'ty': here.ty}, device_id_type=MESH_ID)
                    if sent:
                        copy.wait_send()
                    else:
                        copy.wait_recv()

                if (qd == 0) if kind == 2 else ((qd >> 1, qd & 1)[kind] == 0):
                    pl.when(leaves(slot, qd, kind))(wait)
                else:
                    wait()

    def other(field):
        return jnp.where(field == 0, 0, 3 - field)

    def signed(cond):
        return jnp.where(cond, -1.0, 1.0).astype(F32)

    def pack(field, slot):
        row_idx = [[HALF * h + (63 - (lane >> 2) if k else lane >> 2) for k in PAIR] for h in PAIR]
        plane = lane & 3
        sign_r, sign_c = signed(field == 2), signed(field == 1)
        src_c = other(field)

        def rows_out(t):
            rows = [st[field, slot, w, nat(t), :] for w in range(NW)]
            for h in PAIR:
                for k in PAIR:
                    val = pick(3 - plane if k else plane, [lanes_of(v, row_idx[h][k]) for v in rows])
                    strip[field, slot, 2 * h + k, 0, at(SUBS * t - 30), :] = val * sign_r if k else val

        for t in range(4, 9):
            rows_out(t)
        for w in range(NW):
            turned = jnp.concatenate([st[src_c, slot, w, nat(t), :] for t in range(16)], axis=0).T
            for h in PAIR:
                for k, first, start in ((0, 8, 2 + w), (0, 16, 34 + w), (1, 48, 5 - w), (1, 40, 37 - w)):
                    val = turned[HALF * h + first:HALF * h + first + 8, :]
                    strip[field, slot, 2 * h + k, 1, pl.ds(start, 8, stride=4), :] = rev8(val) * sign_c if k else val
        idx = 69 - (lane & 31)
        for qd in QUADS:
            for ver in PAIR:
                vals = [lanes_of(strip[field, slot, qd, ver, at(8 + SUBS * g), :], idx) for g in QUADS]
                strip_c[field, slot, qd, ver] = pick(lane >> 5, vals)

    def unpack(set_id, field, slot):
        dst_c = other(field)
        row_sign = [signed(field == 1), signed(field >= 1)]
        block_sign = [signed(field >= 1), signed(field == 1)]
        col_sign = [signed(field == 1), signed(field < 0)]
        idx = [jnp.where(lb < 32, 4 * lb + w, 255 - 4 * lb - w) for w in range(NW)]
        for g in QUADS:
            vals = []
            for qd in QUADS:
                face = rbuf[set_id, slot, qd, 0, reg(g), :] * row_sign[qd & 1]
                block = pltpu.roll(rbuf_c[set_id, slot, qd], (6 - 32 * g) % LANES, 1) * block_sign[qd & 1]
                vals.append(rev8(jnp.where(lane < OFF, block, face)))
            for w in range(NW):
                nat_buf[w, at(30 - SUBS * g), :] = pick(lane >> 5, [lanes_of(v, idx[w]) for v in vals])
        for w in range(NW):
            for t in range(5):
                val = nat_buf[w, reg(t), :]
                if t == 0:
                    val = jnp.where(sub >= 6, val, 0.0)
                if t == 4:
                    val = jnp.where(sub < 6, val, st[field, slot, w, nat(t), :])
                st[field, slot, w, nat(t), :] = val
        side_sign = jnp.where(lb < 32, col_sign[0], col_sign[1])
        for w in range(NW):
            low = 1 if w >= 2 else 2
            for h in PAIR:
                turn[w, at(HALF * h + low), :] = rev8(
                    rbuf[set_id, slot, 2 * h, 1, pl.ds((1, 0, 3, 2)[w], 8, stride=4), :])
                turn[w, at(HALF * h + 53 + low), :] = (
                    rbuf[set_id, slot, 2 * h + 1, 1, pl.ds((2, 3, 0, 1)[w], 8, stride=4), :])
            turned = turn[w].T
            inside = ((lb >= low) & (lb < low + 8)) | ((lb >= 53 + low) & (lb < 61 + low))
            first = inside & (sub >= 6)
            for t in range(4, 16):
                st[dst_c, slot, w, nat(t), :] = jnp.where(
                    first if t == 4 else inside, turned[SUBS * t:SUBS * t + 8, :] * side_sign, st[dst_c, slot, w, nat(t), :])

    def vertex_rows(src, slot):
        out_rows = []
        for m in PAIR:
            row = src[slot, 2 + m].T[8:16, :]
            row = pltpu.roll(row, 1, 0)
            vals = []
            for w in range(NW):
                r = (4 * lb + w) & 127
                vals.append(lanes_of(row, 8 * (r & 15) + (r >> 4)))
            out_rows.append(vals)
        return out_rows

    def vertex_cols(src, slot):
        rows = [[src[slot, w, pl.ds(50 + 8 * m, 8, stride=0), :] for w in range(NW)] for m in PAIR]
        return lambda m, v: lanes_of(rows[m][v % 4], 4 * sub + v // 4)

    def row_mask(w):
        return vertex & (sub == 2) & (lane < 10) & (4 * lane + w < OFF)

    def col_mask(v):
        return vertex & (lane == 9) & (sub < (3 if v < 6 else 2))

    def row(ref, pos, idx, plane):
        return pick(plane, [lanes_of(ref[w, at(pos - 1), :], idx) for w in range(NW)])

    def by_column(ref, pos):
        return row(ref, pos, lane >> 2, lane & 3)

    def vertex_setup(slot):
        vals = [by_column(fr[slot], 42), by_column(fr[slot], 50), by_column(kk, 50), by_column(kk, 58)]
        for i in QUADS:
            vcoef[slot, i] = jnp.where(vertex & (sub == 1) & (lane < OFF), vals[i], 0.0)

    def vertex_columns(src, slot):
        rows = [[src[slot, w, pl.ds(50 + 8 * m, 8, stride=0), :] for w in range(NW)] for m in PAIR]

        def ghosts(v):
            for m in PAIR:
                vcol[m, reg(v), :] = lanes_of(rows[m][v % 4], 4 * sub + v // 4)

        return ghosts

    def vertex_turn(src, slot):
        both = jnp.concatenate([src[slot, 2 + m, nat(t), :] for m in PAIR for t in range(5)], axis=0)
        vbuf[0, :, pl.ds(0, 80)] = both[:, :16].T[8:16, :]

    def vertex_gains(slot, s, seven, factor):
        g1 = vbuf[0]
        g2 = pltpu.roll(g1, LANES - 40, 1)
        f1, f2, k1, k2 = [vcoef[slot, i] for i in QUADS]
        inner = s * f2 * g1
        gains = (k1 * (g1 + inner + s * f1 * (seven * g1 - g2)), -k2 * inner)
        for m in PAIR:
            moved = pltpu.roll(factor * gains[m], 1, 0)
            for w in range(NW):
                vrow[m, w] = lanes_of(moved, jnp.where(lane < 32, 4 * lane + w, LANES - 1))

    def vertex_add(dst, slot):
        for m in PAIR:
            for w in range(NW):
                sl = at(48 + 8 * m)
                dst[slot, w, sl, :] = dst[slot, w, sl, :] + vrow[m, w]

    def stage(src, dst, old, slot, s, seven, last):
        end = sub == 7

        def ldx(w, p):
            return src[slot, w, at(p), :]


        def q_row(w, v):
            if v < 0:
                return ldx(w, 8 * (NV + v) - 1)
            if v >= NV:
                return jnp.where(end, pltpu.roll(ldx(w, 8 * (2 * NV - 1 - v)), HALF, 1), ldx(w, 1 + 8 * (v - NV)))
            return ldx(w, SUBS * v)

        def flux_row(w, v):
            pos = SUBS * v if v >= 0 else 8 * (NV + v) - 1
            a, b, c, d = [q_row(w, v + i) for i in (-1, 0, 1, 2)]
            return fr[slot, w, at(pos), :] * ((seven * b - a) + (seven * c - d))

        ghosts = vertex_columns(src, slot)

        def rolls(vs):
            for v in vs:
                ghosts(v)
                q0, q1, q2, q3 = [ldx(w, SUBS * v) for w in range(NW)]
                for i, val in enumerate((pltpu.roll(q3, 1, 1), pltpu.roll(q2, 1, 1), pltpu.roll(q0, LANES - 1, 1),
                                         pltpu.roll(q1, LANES - 1, 1))):
                    roll_buf[i, reg(v), :] = val

        def along_rows(w):
            win = [q_row(w, -1), q_row(w, 0), q_row(w, 1)]
            flux = flux_row(w, -1)
            mid7 = seven * win[1]
            for v in range(NV):
                sl = reg(v)
                b, c, d = win
                n = q_row(w, v + 2)
                d7 = seven * d
                f = fr[slot, w, sl, :] * ((mid7 - b) + (d7 - n))
                row_buf[w, sl, :] = (b + d) - s * (f - flux)
                flux, mid7, win = f, d7, [c, d, n]

        def along_cols(v):
            sl = reg(v)
            q = [ldx(w, SUBS * v) for w in range(NW)]
            for m in PAIR:
                q[1 - m] = jnp.where(col_mask(v), vcol[m, sl, :], q[1 - m])
            qm1, qm2, q4, q5 = [roll_buf[i, sl, :] for i in QUADS]
            q7 = [seven * x for x in q]
            left = [q7[w] - (q[w - 1] if w else qm1) for w in range(NW)]
            right = [q7[w] - (q[w + 1] if w < 3 else q4) for w in range(NW)] + [seven * q4 - q5]
            g_prev = fcm[slot, sl, :] * ((seven * qm1 - qm2) + right[0])
            for w in range(NW):
                g = fc[slot, w, sl, :] * (left[w] + right[w + 1])
                sum_col = (q[w - 1] if w else qm1) + (q[w + 1] if w < 3 else q4)
                gain = (row_buf[w, sl, :] + sum_col) - s * (g - g_prev)
                val = mm[w, sl, :] * q[w] + kk[w, sl, :] * gain
                if last:
                    val = 0.5 * (val + old[slot, w, sl, :])
                dst[slot, w, sl, :] = val
                g_prev = g

        vertex_turn(src, slot)
        rolls(range(NV))
        for w in range(NW):
            along_rows(w)
        vertex_gains(slot, s, seven, 0.5 if last else 1.0)
        for v in range(NV):
            along_cols(v)
        vertex_add(dst, slot)

    xa, wr, wc = st.at[0], st.at[1], st.at[2]

    def load():
        low_rows = half == here.ftx
        cols = [4 * lb + w - OFF for w in range(NW)]
        cols = [c + here.fty * (size - 1 - 2 * c) for c in cols]
        flip_col = signed(here.fty == 1)

        def window(t):
            for field in range(3):
                for slot in range(slots):
                    low, high = [in_ref[field, slot, at(pl.multiple_of(first, 8)), :]
                                 for first in (SUBS * t, size + 68 - SUBS * t)]
                    low, high = [low[:, :LANES], low[:, LANES:]], [rev8(high[:, :LANES]), rev8(high[:, LANES:])]
                    for w in range(NW):
                        idx = cols[w] & (LANES - 1)
                        part = [jnp.where(cols[w] < LANES, lanes_of(x[0], idx), lanes_of(x[1], idx)) for x in (low, high)]
                        val = jnp.where(low_rows, part[0], -part[1] if field == 1 else part[1])
                        st[field, slot, w, nat(t), :] = val * flip_col if field == 2 else val

        for field in range(3):
            for slot in range(slots):
                for w in range(NW):
                    for t in QUADS:
                        st[field, slot, w, nat(t), :] = jnp.zeros((SUBS, LANES), F32)
        loop(16, window, 4)

    def faces(slot):
        cst = 0.5 / 12.0 / (0.5 * C_SPEED)
        rows = vertex_rows(wc, slot)
        cols = vertex_cols(wr, slot)
        for w in range(NW):
            sl = at(40)
            wr[slot, w, sl, :] = jnp.where(row_mask(w), -rows[0][w], wr[slot, w, sl, :])
        for v in range(NV):
            sl = reg(v)
            wc[slot, 1, sl, :] = jnp.where(col_mask(v), -cols(0, v), wc[slot, 1, sl, :])

        def plane(w):
            for v in range(NV):
                sl = reg(v)
                here_w = wr[slot, w, sl, :]
                if v < NV - 1:
                    next_w = wr[slot, w, at(SUBS * v + 8), :]
                else:
                    next_w = jnp.where(sub == 7, -pltpu.roll(here_w, HALF, 1), wr[slot, w, at(1), :])
                fr[slot, w, sl, :] = cst * (here_w + next_w)

        loop(NW, plane)
        for v in range(NV):
            sl = reg(v)
            col = [wc[slot, w, sl, :] for w in range(NW)]
            col.append(pltpu.roll(col[0], LANES - 1, 1))
            for w in range(NW):
                val = cst * (col[w] + col[w + 1])
                fc[slot, w, sl, :] = val
            fcm[slot, sl, :] = pltpu.roll(val, 1, 1)

    def store(t):
        for slot in range(slots):
            rows = [st[0, slot, w, nat(t), :] for w in range(NW)]
            for top in PAIR:
                own_half = here.ftx + top * (1 - 2 * here.ftx)
                for part in PAIR:
                    col = lane + LANES * part
                    col = (col + here.fty * (size - 1 - 2 * col) + OFF) & 255
                    val = pick(col & 3, [lanes_of(v, HALF * own_half + (col >> 2)) for v in rows])
                    first = pl.multiple_of(size + 68 - SUBS * t if top else SUBS * t, 8)
                    out[slot, at(first), pl.ds(LANES * part, LANES)] = rev8(val) if top else val

    def clear(slot):
        def one(set_id):
            for qd in QUADS:
                rbuf_c[set_id, slot, qd] = jnp.zeros((SUBS, LANES), F32)
        loop(4, one)

    loop(slots, clear)
    vbuf[...] = jnp.zeros(vbuf.shape, F32)
    barrier = pltpu.get_barrier_semaphore()

    peers = 0
    for slot in range(slots):
        for qd in QUADS:
            for kind in range(3):
                device, _, _, _, stays = to(slot, qd, kind)

                @pl.when(jnp.logical_not(stays))
                def _():
                    pl.semaphore_signal(barrier, 1, device_id=device, device_id_type=MESH_ID)

                peers = peers + jnp.where(stays, 0, 1)

    for w in range(NW):
        for v in range(NV):
            sl = reg(v)
            corner = vertex & (lane < 10) & (4 * lane + w < OFF) & (16 * sub + v < OFF)
            val = jnp.where(corner, 0.0, k_in[w, sl, :])
            kk[w, sl, :] = val
            mm[w, sl, :] = jnp.where(val == 0.0, 0.0, 1.0 - 4.0 * val)
    load()
    pl.semaphore_wait(barrier, peers)

    def first_send(field):
        def one(slot):
            pack(field, slot)
            send(field, jnp.where(field == 0, 0, field + 1), slot)
        loop(slots, one)

    loop(3, first_send)

    def wind_halos(slot):
        def one(field):
            wait_all(field, field + 1, slot, False)
            wait_all(field, field + 1, slot, True)
            unpack(field + 1, field, slot)
        loop(3, one, 1)
        faces(slot)
        vertex_setup(slot)

    loop(slots, wind_halos)

    def slot_of(i):
        if tiles * tiles * 2 != len(ORDER_OF) or slots != 3:
            return i
        at = (here.pd * tiles + here.tx) * tiles + here.ty
        code = jnp.int32(0)
        for name, order in ORDERS.items():
            value = sum(int(slot) << (2 * i) for i, slot in enumerate(order))
            for pos, other_name in enumerate(ORDER_OF):
                if other_name == name:
                    code = jnp.where(at == pos, value, code)
        return (code >> (2 * i)) & 3

    def one_round(rnd):
        def one_slot(slot):
            set_id = rnd & 1
            wait_all(0, set_id, slot, False)
            unpack(set_id, 0, slot)

            def one_step(t):
                s = ws[rnd * STEPS_PER_ROUND + t]
                seven = ws[steps]
                stage(xa, xb, xa, slot, s, seven, False)
                stage(xb, xa, xa, slot, s, seven, True)

            loop(STEPS_PER_ROUND, one_step)
            wait_all(0, 0, slot, True)

            @pl.when(rnd < rounds - 1)
            def _():
                pack(0, slot)
                send(0, 1 - set_id, slot)

        loop(slots, lambda i: one_slot(slot_of(i)))

    loop(rounds, one_round)
    loop(16, store, 4)


def metric(tiles, size):
    cells = tiles * size
    step = 0.5 * math.pi / cells
    row = jnp.arange(LANES)
    row = 16 * (row % 8) + row // 8
    halves = jnp.arange(2)
    flip_x = lax.axis_index('tx') // (tiles // 2)
    flip_y = lax.axis_index('ty') // (tiles // 2)

    def square(pos, first):
        pos = pos + first * size
        pos = jnp.where(pos < 0, -1 - pos, pos)
        pos = jnp.where(pos >= cells, 2 * cells - 1 - pos, pos)
        tan = jnp.tan((pos.astype(F32) + 0.5) * step - 0.25 * math.pi)
        return tan * tan

    own = row[:, None] - OFF
    is_high = (halves[None, :] + flip_x) % 2
    sq_a = square(jnp.where(is_high == 1, size - 1 - own, own), lax.axis_index('tx'))
    sq_a = jnp.repeat(sq_a, HALF, axis=1)[None]
    col = 4 * jnp.arange(HALF)[None, :] + jnp.arange(NW)[:, None]
    own = col - OFF
    sq_b = square(jnp.where(flip_y == 1, size - 1 - own, own), lax.axis_index('ty'))
    sq_b = jnp.tile(sq_b, (1, 2))[:, None, :]
    r_sq = 1.0 + sq_a + sq_b
    val = (0.5 * C_SPEED * CFL_STEP) * (r_sq * jnp.sqrt(r_sq)) / ((1.0 + sq_a) * (1.0 + sq_b))
    first = OFF - HALO
    col = jnp.tile(col, (1, 2))[:, None, :]
    real = (row[None, :, None] >= first) & (col >= first) & (col < 4 * HALF - first)
    return jnp.where(real, val, 0.0)


def solution(mesh):
    tiles = mesh.shape['tx']
    slots = 6 // mesh.shape['panel']
    field_spec = P(('member', 'panel'), 'tx', 'ty')
    wind_spec = P('panel', 'tx', 'ty')

    def local_run(tracer, wind_a, wind_b, wind_scale):
        size = tracer.shape[1]
        steps = wind_scale.shape[0]
        padded = jnp.stack([jnp.pad(x, ((0, 0), (OFF, 6), (0, 2 * LANES - size))) for x in (tracer, wind_a, wind_b)])
        scale = jnp.concatenate([wind_scale, jnp.full((8,), 7.0, F32)])
        vmem = pl.BlockSpec(memory_space=pltpu.VMEM)
        planes = pltpu.VMEM((slots, NW, LANES, LANES), F32)
        quad = (slots, 4)
        return pl.pallas_call(
            functools.partial(kernel, tiles, steps, size),
            out_shape=jax.ShapeDtypeStruct((slots, size + OFF + 6, 2 * LANES), F32),
            in_specs=[pl.BlockSpec(memory_space=pltpu.SMEM)] + [vmem] * 2,
            out_specs=vmem,
            scratch_shapes=[
                pltpu.VMEM((3, slots, NW, LANES, LANES), F32), planes, planes, planes,
                pltpu.VMEM((slots, LANES, LANES), F32),
                pltpu.VMEM((NW, LANES, LANES), F32), pltpu.VMEM((NW, LANES, LANES), F32),
                pltpu.VMEM((slots, 4, 8, LANES), F32),
                pltpu.VMEM((4, 8, LANES), F32), pltpu.VMEM((2, LANES, LANES), F32), pltpu.VMEM((2, NW, 8, LANES), F32),
                pltpu.VMEM((4, LANES, LANES), F32), pltpu.VMEM((NW, LANES, LANES), F32),
                pltpu.VMEM((NW, HALF, LANES), F32),
                pltpu.VMEM((NW, LANES, LANES), F32),
                pltpu.VMEM((3, *quad, 2, 96, LANES), F32),
                pltpu.VMEM((3, *quad, 2, 8, LANES), F32),
                pltpu.VMEM((4, *quad, 2, HALO, LANES), F32),
                pltpu.VMEM((4, *quad, 8, LANES), F32),
                pltpu.SemaphoreType.DMA((3, *quad, 3)),
                pltpu.SemaphoreType.DMA((4, *quad, 3)),
            ],
            compiler_params=pltpu.CompilerParams(collective_id=0, has_side_effects=True, vmem_limit_bytes=60 * 2**20),
        )(scale, padded, metric(tiles, size))[:, OFF:OFF + size, :size]

    return jax.shard_map(local_run, mesh=mesh, in_specs=(field_spec, wind_spec, wind_spec, P()),
                         out_specs=field_spec, check_vma=False)
```

time: 10700 us -> 196 us (0.02); the launches traced: 10600 us -> 195 us
  starting transfers between devices: 6240 us -> 0 us
  waiting for transfers between devices: 2070 us -> 0 us
  local copies, waits for them, and re-layouts: 1210 us -> 4.96 us
  other arithmetic: 952 us -> 2.56 us
  Pallas kernels: 0 us -> 187 us
    ppermute x3612 -> x0, starting transfers between devices: 6240 us -> none  [the longest x3096 5000 us: fill_halo(): moved_strip = lax.ppermute(one_strip, group_axes, perm_pairs)]
    ppermute x3612 -> x0, waiting for transfers between devices: 2070 us -> none  [the longest x3096 2070 us: fill_halo(): moved_strip = lax.ppermute(one_strip, group_axes, perm_pairs)]
    rev x835 -> x0, local copies, waits for them, and re-layouts: 518 us -> none  [the longest x448 380 us: fill_halo(): one_strip = jnp.flip(one_strip, axis=1)]
    another operation x1742 -> x1, other arithmetic: 411 us -> 1.47 us  [local_run(): jnp.stack([jnp.pad(x, ((0, 0), (OFF, 6), (0, 2 * LANES - size))) for x in...]
    sub x256 -> x1, other arithmetic: 311 us -> 0.01 us  [metric(): own = row[:, None] - OFF]
    while x2944 -> x0, local copies, waits for them, and re-layouts: 252 us -> none
    add x645 -> x2, other arithmetic: 191 us -> 0.13 us  [the longest x1 0.13 us: metric(): r_sq = 1.0 + sq_a + sq_b]
    pallas_call x0 -> x1, Pallas kernels: none -> 187 us  [local_run(): pl.pallas_call(functools.partial(kernel, tiles, steps, size), out_shape=j...]
where the time goes in v1:
time: 196 us; the launch traced here: 195 us
  Pallas kernels  187 us (95%)
  local copies, waits for them, and re-layouts  4.96 us (3%)
  other arithmetic  2.56 us (1%)
    pallas_call x1, Pallas kernels, local_run(): pl.pallas_call(functools.partial(kernel, tiles, steps, size), out_shape=j...  187 us

profile of v1, /device:TPU:97, one launch (start us, length us, event | category | flops | bytes accessed | tf_op | source)
XLA Modules:
  0.0 194.7 jit_solution(9162765690577618749)
XLA Ops:
  0.0 0.0 copy-start
  0.0 1.3 concatenate.3.ws
  1.3 1.3 pad_bitcast_fusion
  2.6 0.0 copy-done
  2.6 0.1 pad_bitcast_fusion.2
  2.7 1.5 pad_maximum_fusion.in_ref
  4.2 0.1 fusion.9
  4.2 0.1 tile.19
  4.4 0.1 fusion.18
  4.5 0.1 copy.5
  4.6 0.1 lt.50
  4.7 0.1 ge.46
  4.8 0.9 fusion.2.k_in
  5.7 187.1 %shard_map.46 = f32[3,224,256]{2,1,0:T(8,128)} custom-call(f32[72]{0:T(128)} %concatenate.3.ws, f32[3,3,224,256]{3,2,1,0:T(8,128)} %pad_maximum_fusion.in_ref, f32[4,128,128]{2,1,0:T(8,128)} %fusion.2.k_in), custom_call_target="tpu_custom_call" | custom-call | tf_op jit(solution)/shard_map/pallas_call | solution.py:629
  192.8 1.9 slice.3
  (10 shorter events, 0.1 us)
Async XLA Ops:
  0.0 2.6 %copy-start = (f32[3,180,180]{2,1,0:T(8,128)S(1)}, f32[3,180,180]{2,1,0:T(8,128)}, u32[]{:S(2)}) copy-start(f32[3,180,180]{2,1,0:T(8,128)} %param.4) | copy-start | bytes 1166404

commit v2 on v1

v2 whole, which is shorter than its diff:
```python
import functools
import math
import jax
import jax.numpy as jnp
from jax import lax
from jax.experimental import pallas as pl
from jax.experimental.pallas import tpu as pltpu
from jax.sharding import PartitionSpec as P

C_SPEED = 2.5
CFL_STEP = 0.12
EDGES = ('310,100,530,420', '010,200,511,410', '110,300,521,431', '210,000,500,401', '331,130,030,231', '320,121,221,020')
EDGE_TABLE = [[[int(digit) for digit in side] for side in panel.split(',')] for panel in EDGES]

LANES = 128
NV = 16
NW = 4
OFF = 38
HALO = 32
STEPS_PER_ROUND = 8
NIBBLE = 4
SUBS = 8
VROW = 49
HALF = 64
UNROLL = 4
PAIR = range(2)
QUADS = range(4)
ORDERS = {'a': '210', 'b': '201', 'c': '120', 'd': '102'}
ORDER_OF = 'abbbaaaacccccccc' + 'bacdbacdbacdaacd'
F32 = jnp.float32
I32 = jnp.int32
MESH_ID = pl.DeviceIdType.MESH


def lane_id():
    return lax.broadcasted_iota(I32, (SUBS, LANES), 1)


def sub_id():
    return lax.broadcasted_iota(I32, (SUBS, LANES), 0)


def lanes_of(val, idx):
    return jnp.take_along_axis(val, idx, axis=1, mode="promise_in_bounds")


def rev8(val):
    return jnp.take_along_axis(val, 7 - sub_id(), axis=0, mode="promise_in_bounds")


def pick(sel, vals):
    if isinstance(sel, int):
        return vals[sel]
    out = vals[-1]
    for i in range(len(vals) - 2, -1, -1):
        out = jnp.where(sel == i, vals[i], out)
    return out


def reg(v):
    return pl.ds(SUBS * v, SUBS)


def at(pos):
    return pl.ds(pos, SUBS)


def nat(t):
    return pl.ds(HALF * (t & 1) + (t >> 1), 8, stride=8)


class Where:
    def __init__(self, tiles, panels_per_dev):
        self.n, self.lp = tiles, panels_per_dev
        self.tx, self.ty, self.pd = lax.axis_index('tx'), lax.axis_index('ty'), lax.axis_index('panel')
        self.ftx, self.fty = self.flip(self.tx), self.flip(self.ty)
        self.edge_x = self.at_edge(self.tx)
        self.edge_y = self.at_edge(self.ty)
        self.vertex = self.edge_x * self.edge_y

    def flip(self, t):
        return lax.div(t, jnp.int32(self.n // 2))

    def at_edge(self, t):
        return jnp.where(t == 0, 1, jnp.where(t == self.n - 1, 1, 0))

    @staticmethod
    def xor(a, b):
        return a + b - 2 * a * b

    def lookup(self, slot, base, bit):
        near, far = [[np_ * SUBS + e * 2 + fl for np_, e, fl in EDGE_TABLE[slot + d * self.lp][base:base + 2]] for d in PAIR]
        low = near[0] + bit * (near[1] - near[0])
        return low + self.pd * (far[0] + bit * (far[1] - far[0]) - low)

    def cross(self, slot, base, bit, along, along_half):
        code = self.lookup(slot, base, bit)
        np_, e, fl = code >> 3, (code >> 1) & 3, code & 1
        al = along + fl * (self.n - 1 - 2 * along)
        alh = self.xor(along_half, fl)
        col, end = e >> 1, e & 1
        far = end * (self.n - 1)
        tx = far + col * (al - far)
        ty = al + col * (far - al)
        hp = end + col * (alh - end)
        kp = alh + col * (end - alh)
        pd = lax.div(np_, jnp.int32(self.lp))
        return (pd, np_ - pd * self.lp, tx, ty, self.xor(hp, self.flip(tx)), self.xor(kp, self.flip(ty)), col)

    def mix(self, flag, a, b):
        return tuple(x + flag * (y - x) for x, y in zip(a, b))

    def face(self, slot, h, k, kind):
        hp, kp = self.xor(h, self.ftx), self.xor(k, self.fty)
        if kind == 0:
            tx = self.tx + 2 * hp - 1
            inner = (self.pd, slot, tx, self.ty, self.xor(1 - hp, self.flip(tx)), k, 0)
            return inner if h else self.mix(self.edge_x, inner, self.cross(slot, 0, hp, self.ty, kp))
        ty = self.ty + 2 * kp - 1
        inner = (self.pd, slot, self.tx, ty, h, self.xor(1 - kp, self.flip(ty)), 1)
        return inner if k else self.mix(self.edge_y, inner, self.cross(slot, 2, kp, self.tx, hp))

    def corner(self, slot, h, k):
        hp, kp = self.xor(h, self.ftx), self.xor(k, self.fty)
        tx, ty = self.tx + 2 * hp - 1, self.ty + 2 * kp - 1
        dest = (self.pd, slot, tx, ty, self.xor(1 - hp, self.flip(tx)), self.xor(1 - kp, self.flip(ty)), 0)
        if not k:
            d = self.cross(slot, 2, kp, tx, 1 - hp)
            dest = self.mix(self.edge_y, dest, d[:6] + (1 - d[6],))
        if not h:
            dest = self.mix(self.edge_x, dest, self.cross(slot, 0, hp, ty, 1 - kp))
        return dest


def kernel(tiles, steps, size, ws, q_in, wa_in, wb_in, k_in, out, tile_buf, st, xb, fr, fc, fcm, kk, row_scaled, col_scaled, vcoef, vturn, vback, roll_buf, row_buf, nat_buf, turn,
           strip, strip_c, rbuf, rbuf_c, send_sem, recv_sem):
    slots = out.shape[0]
    lane, sub = lane_id(), sub_id()
    lb, half = lane & 63, lane >> 6
    here = Where(tiles, slots)
    rounds = steps // STEPS_PER_ROUND
    vertex = here.vertex == 1
    xa, wr, wc = st.at[0], st.at[1], st.at[2]

    def loop(count, fn, first=0):
        def body(i, carry):
            fn(i)
            return carry
        lax.fori_loop(first, count, body, 0)

    def plan(slot, qd, kind):
        h, k = qd >> 1, qd & 1
        dest = here.corner(slot, h, k) if kind == 2 else here.face(slot, h, k, kind)
        code = dest[0]
        for i, part in enumerate((dest[1], dest[2], dest[3], 2 * dest[4] + dest[5], dest[6])):
            code = code + (part << (NIBBLE * (i + 1)))
        if kind == 2:
            if qd:
                return code
            stays = vertex
        elif (h, k)[kind]:
            return code
        else:
            stays = (dest[0] == here.pd) & (dest[2] == here.tx) & (dest[3] == here.ty)
        return code + jnp.where(stays, 1 << (6 * NIBBLE), 0)

    plans = [[[plan(slot, qd, kind) for kind in range(3)] for qd in QUADS] for slot in range(slots)]

    def code_of(slot, qd, kind):
        return pick(slot, [plans[i][qd][kind] for i in range(slots)])

    def to(slot, qd, kind):
        code = code_of(slot, qd, kind)
        pd, slot2, tx, ty, qd2, kind2 = [(code >> (NIBBLE * i)) & ((1 << NIBBLE) - 1) for i in range(6)]
        return {'panel': pd, 'tx': tx, 'ty': ty}, slot2, qd2, kind2, (code >> (6 * NIBBLE)) == 1

    def leaves(slot, qd, kind):
        return (code_of(slot, qd, kind) >> (6 * NIBBLE)) == 0

    def send(field, set_id, slot):
        for qd in QUADS:
            for kind in range(3):
                device, slot2, qd2, kind2, stays = to(slot, qd, kind)
                if kind < 2:
                    src, dst = strip.at[field, slot, qd, kind, pl.ds(SUBS, HALO)], rbuf.at[set_id, slot2, qd2, kind2]
                    sem = recv_sem.at[set_id, slot2, qd2, kind2]
                else:
                    src, dst = strip_c.at[field, slot, qd, kind2], rbuf_c.at[set_id, slot2, qd2]
                    sem = recv_sem.at[set_id, slot2, qd2, 2]

                @pl.when(jnp.logical_not(stays))
                def _():
                    pltpu.make_async_remote_copy(
                        src_ref=src, dst_ref=dst, send_sem=send_sem.at[field, slot, qd, kind], recv_sem=sem,
                        device_id=device, device_id_type=MESH_ID).start()

                if kind < 2 and (qd >> 1, qd & 1)[kind] == 0:
                    @pl.when(stays)
                    def _():
                        for g in QUADS:
                            rbuf[set_id, slot2, qd2, kind2, reg(g), :] = (
                                strip[field, slot, qd, kind, at(8 + SUBS * g), :])

    def wait_all(field, set_id, slot, sent):
        for qd in QUADS:
            for kind in range(3):
                if kind < 2:
                    src, dst = strip.at[field, slot, qd, kind, pl.ds(SUBS, HALO)], rbuf.at[set_id, slot, qd, kind]
                else:
                    src, dst = strip_c.at[field, slot, qd, 0], rbuf_c.at[set_id, slot, qd]

                def wait():
                    copy = pltpu.make_async_remote_copy(
                        src_ref=src, dst_ref=dst, send_sem=send_sem.at[field, slot, qd, kind],
                        recv_sem=recv_sem.at[set_id, slot, qd, kind],
                        device_id={'panel': here.pd, 'tx': here.tx, 'ty': here.ty}, device_id_type=MESH_ID)
                    if sent:
                        copy.wait_send()
                    else:
                        copy.wait_recv()

                if (qd == 0) if kind == 2 else ((qd >> 1, qd & 1)[kind] == 0):
                    pl.when(leaves(slot, qd, kind))(wait)
                else:
                    wait()

    def other(field):
        return jnp.where(field == 0, 0, 3 - field)

    def signed(cond):
        return jnp.where(cond, -1.0, 1.0).astype(F32)

    def pack(field, slot):
        sign_r, sign_c = signed(field == 2), signed(field == 1)
        src_c = other(field)
        line = lax.broadcasted_iota(I32, (5 * SUBS, LANES), 1)
        plane = line & 3
        rows = [jnp.concatenate([st[field, slot, w, nat(t), :] for t in range(4, 9)], axis=0) for w in range(NW)]
        for h in PAIR:
            for k in PAIR:
                idx = HALF * h + (HALF - 1 - (line >> 2) if k else line >> 2)
                val = pick(3 - plane if k else plane, [lanes_of(v, idx) for v in rows])
                strip[field, slot, 2 * h + k, 0, pl.ds(2, 5 * SUBS), :] = val * sign_r if k else val
        for w in range(NW):
            turned = jnp.concatenate([st[src_c, slot, w, nat(t), :] for t in range(16)], axis=0).T
            for h in PAIR:
                for k, first, start in ((0, 8, 2 + w), (0, 16, 34 + w), (1, 48, 5 - w), (1, 40, 37 - w)):
                    val = turned[HALF * h + first:HALF * h + first + SUBS, :]
                    strip[field, slot, 2 * h + k, 1, pl.ds(start, SUBS, stride=4), :] = rev8(val) * sign_c if k else val
        line = lax.broadcasted_iota(I32, (HALO, LANES), 1)
        for qd in QUADS:
            for ver in PAIR:
                val = lanes_of(strip[field, slot, qd, ver, pl.ds(SUBS, HALO), :], 69 - (line & 31))
                strip_c[field, slot, qd, ver] = pick(lane >> 5, [val[SUBS * g:SUBS * g + SUBS] for g in QUADS])

    def unpack(set_id, field, slot):
        dst_c = other(field)
        row_sign = [signed(field == 1), signed(field >= 1)]
        block_sign = [signed(field >= 1), signed(field == 1)]
        col_sign = [signed(field == 1), signed(field < 0)]
        line = lax.broadcasted_iota(I32, (HALO, LANES), 1)
        near = line & (HALF - 1)
        vals = []
        for qd in QUADS:
            parts = []
            for g in reversed(QUADS):
                face = rbuf[set_id, slot, qd, 0, reg(g), :] * row_sign[qd & 1]
                block = pltpu.roll(rbuf_c[set_id, slot, qd], (6 - 32 * g) % LANES, 1) * block_sign[qd & 1]
                parts.append(rev8(jnp.where(lane < OFF, block, face)))
            vals.append(jnp.concatenate(parts, axis=0))
        for w in range(NW):
            idx = jnp.where(near < 32, 4 * near + w, 255 - 4 * near - w)
            nat_buf[w, pl.ds(OFF - HALO, HALO), :] = pick(line >> 5, [lanes_of(v, idx) for v in vals])
        for w in range(NW):
            for t in range(5):
                val = nat_buf[w, reg(t), :]
                if t == 0:
                    val = jnp.where(sub >= 6, val, 0.0)
                if t == 4:
                    val = jnp.where(sub < 6, val, st[field, slot, w, nat(t), :])
                st[field, slot, w, nat(t), :] = val
        side_sign = jnp.where(lb < 32, col_sign[0], col_sign[1])
        for w in range(NW):
            low = 1 if w >= 2 else 2
            for h in PAIR:
                turn[w, at(HALF * h + low), :] = rev8(
                    rbuf[set_id, slot, 2 * h, 1, pl.ds((1, 0, 3, 2)[w], 8, stride=4), :])
                turn[w, at(HALF * h + 53 + low), :] = (
                    rbuf[set_id, slot, 2 * h + 1, 1, pl.ds((2, 3, 0, 1)[w], 8, stride=4), :])
            turned = turn[w].T
            inside = ((lb >= low) & (lb < low + 8)) | ((lb >= 53 + low) & (lb < 61 + low))
            first = inside & (sub >= 6)
            for t in range(4, 16):
                st[dst_c, slot, w, nat(t), :] = jnp.where(
                    first if t == 4 else inside, turned[SUBS * t:SUBS * t + 8, :] * side_sign, st[dst_c, slot, w, nat(t), :])

    def col_mask(v):
        return vertex & (lane == 9) & (sub < (3 if v < 4 else 2))

    def near_vertex(w):
        return vertex & (sub == 1) & (lane < OFF // NW + 1) & (NW * lane + w < OFF)

    def vertex_setup(slot):
        for w in range(NW):
            near = near_vertex(w)
            vals = [fr[slot, w, at(VROW - SUBS), :], fr[slot, w, at(VROW), :], kk[w, at(VROW), :], kk[w, at(VROW + SUBS), :]]
            for i, val in enumerate(vals):
                vcoef[slot, w, i] = jnp.where(near, val, 0.0)

    def vertex_turn(src, slot):
        for m in PAIR:
            for w in range(NW):
                for i in range(NW):
                    vturn[m, w, pl.ds(i, SUBS, stride=NW), :] = src[slot, 2 + m, reg(NW * i + w), :]
                vturn[m, w, pl.ds(9, 1), pl.ds(0, 9)] = src[slot, w, pl.ds(VROW + 1 + SUBS * m, 1), pl.ds(0, 9)]
        for m in PAIR:
            for w in range(NW):
                vback[m, w, pl.ds(0, NV), pl.ds(0, NV)] = vturn[m, w, :NV, :NV].T

    def vertex_column(src, slot, m, v, own):
        i, w = v // NW, v % NW
        val = jnp.where(col_mask(v), vback[m, w, pl.ds(i, SUBS, stride=NW), :], own)
        if v in (4, 5):
            val = jnp.where(vertex & (lane == 9) & (sub == 2), src[slot, w, reg(6 + m), :], val)
        return val

    def vertex_add(dst, slot, s, seven, factor):
        for w in range(NW):
            g1, g2 = vback[0, w, reg(1), :], vback[1, w, reg(1), :]
            f1, f2, k1, k2 = [vcoef[slot, w, i] for i in QUADS]
            inner = s * f2 * g1
            gains = (k1 * (g1 + inner + s * f1 * (seven * g1 - g2)), -k2 * inner)
            for m in PAIR:
                sl = at(VROW + SUBS * m)
                dst[slot, w, sl, :] = dst[slot, w, sl, :] + (factor * gains[m] if factor != 1 else gains[m])

    def stage(src, dst, old, slot, s, seven, last):
        def row_wind(pos):
            return row_scaled[:, at(pos), :] if last else s * fr[slot, :, at(pos), :]

        def q_row(v):
            if v < 0:
                return src[slot, :, at(SUBS * (NV + v) - 1), :]
            if v < NV:
                return src[slot, :, reg(v), :]
            beyond = pltpu.roll(src[slot, :, reg(2 * NV - 1 - v), :], HALF, 2)
            return jnp.where(sub[None] == SUBS - 1, beyond, src[slot, :, at(1 + SUBS * (v - NV)), :])

        def along_rows():
            a, b, c, d = [q_row(i - 2) for i in QUADS]
            mid7 = seven * c
            flux = (c - b) - row_wind(SUBS * NV - SUBS - 1) * ((seven * b - a) + (mid7 - d))
            for v in range(NV):
                b, c, d = (b, c, d) if v == 0 else (c, d, n)
                n = q_row(v + 2)
                d7 = seven * d
                wind = row_wind(SUBS * v)
                if not last:
                    row_scaled[:, reg(v), :] = wind
                f = (d - c) - wind * ((mid7 - b) + (d7 - n))
                row_buf[:, reg(v), :] = f - flux
                flux, mid7 = f, d7

        def chain(*parts):
            return jnp.concatenate([x if x.ndim == 3 else x[None] for x in parts], axis=0)

        def along_cols(v):
            sl = reg(v)
            own = src[slot, :, sl, :]
            q = chain(*[vertex_column(src, slot, 1 - m, v, own[m]) for m in PAIR], own[2:])
            qm2, qm1, q4, q5 = [roll_buf[i, sl, :] for i in QUADS]
            q7 = seven * q
            up = chain(q[1:], q4)
            left, right = q7 - chain(qm1, q[:3]), q7 - up
            if last:
                wind, first_wind = col_scaled[:NW, sl, :], col_scaled[NW, sl, :]
            else:
                wind, first_wind = s * fc[slot, :, sl, :], s * fcm[slot, sl, :]
                col_scaled[:NW, sl, :] = wind
                col_scaled[NW, sl, :] = first_wind
            g = (up - q) - wind * (left + chain(right[1:], seven * q4 - q5))
            first = (q[0] - qm1) - first_wind * ((seven * qm1 - qm2) + right[0])
            val = own + kk[:, sl, :] * (row_buf[:, sl, :] + (g - chain(first, g[:3])))
            dst[slot, :, sl, :] = 0.5 * (val + old[slot, :, sl, :]) if last else val

        vertex_turn(src, slot)
        for v in range(NV):
            q = src[slot, :, reg(v), :]
            roll_buf[:2, reg(v), :] = pltpu.roll(q[2:], 1, 2)
            roll_buf[2:, reg(v), :] = pltpu.roll(q[:2], LANES - 1, 2)
        along_rows()
        for v in range(NV):
            along_cols(v)
        vertex_add(dst, slot, s, seven, 0.5 if last else 1)


    inside = pl.ds(OFF, size)
    rest = size - LANES

    def rows_in(slot):
        for field, ref in enumerate((q_in, wa_in, wb_in)):
            tile_buf[field, slot, 0, inside, :] = ref[slot, :, pl.ds(0, LANES)]
            tile_buf[field, slot, 1, inside, pl.ds(0, rest)] = ref[slot, :, pl.ds(LANES, rest)]

    def rows_out(slot):
        out[slot, :, pl.ds(0, LANES)] = tile_buf[0, slot, 0, inside, :]
        out[slot, :, pl.ds(LANES, rest)] = tile_buf[0, slot, 1, inside, pl.ds(0, rest)]

    def load():
        low_rows = half == here.ftx
        cols = [4 * lb + w - OFF for w in range(NW)]
        cols = [c + here.fty * (size - 1 - 2 * c) for c in cols]
        flip_col = signed(here.fty == 1)

        tall = [jnp.concatenate([x] * (3 * slots), axis=0) for x in (*cols, low_rows.astype(I32))]

        def window(t):
            low, high = [[tile_buf[:, :, part, at(pl.multiple_of(first, SUBS)), :] for part in PAIR]
                         for first in (SUBS * t, size + 68 - SUBS * t)]
            low = [x.reshape(3 * slots * SUBS, LANES) for x in low]
            high = [jnp.concatenate([rev8(x[f, i]) * (-1.0 if f == 1 else 1.0) for f in range(3) for i in range(slots)], axis=0)
                    for x in high]
            for w in range(NW):
                idx = tall[w] & (LANES - 1)
                part = [jnp.where(tall[w] < LANES, lanes_of(x[0], idx), lanes_of(x[1], idx)) for x in (low, high)]
                val = jnp.where(tall[NW] == 1, part[0], part[1])
                for i in range(3 * slots):
                    field, one = divmod(i, slots)
                    piece = val[SUBS * i:SUBS * i + SUBS]
                    st[field, one, w, nat(t), :] = piece * flip_col if field == 2 else piece

        def blank(slot):
            for field in range(3):
                for w in range(NW):
                    for t in QUADS:
                        st[field, slot, w, nat(t), :] = jnp.zeros((SUBS, LANES), F32)

        loop(slots, blank)
        loop(slots, rows_in)
        loop(16, window, 4)

    def faces(slot):
        cst = 0.5 / 12.0 / (0.5 * C_SPEED)
        vertex_turn(wc, slot)
        for w in range(NW):
            sl = at(VROW - SUBS)
            wr[slot, w, sl, :] = jnp.where(near_vertex(w), -vback[0, w, reg(1), :], wr[slot, w, sl, :])
        vertex_turn(wr, slot)
        for v in range(SUBS):
            for u in (v, v + SUBS):
                wc[slot, 1, reg(u), :] = -vertex_column(wr, slot, 0, u, -wc[slot, 1, reg(u), :])

        def row_faces(v):
            for w in range(NW):
                fr[slot, w, reg(v), :] = cst * (wr[slot, w, reg(v), :] + wr[slot, w, reg(v + 1), :])

        def col_faces(v):
            col = [wc[slot, w, reg(v), :] for w in range(NW)]
            col.append(pltpu.roll(col[0], LANES - 1, 1))
            for w in range(NW):
                val = cst * (col[w] + col[w + 1])
                fc[slot, w, reg(v), :] = val
            fcm[slot, reg(v), :] = pltpu.roll(val, 1, 1)

        loop(NV - 1, row_faces)
        for w in range(NW):
            inner = wr[slot, w, reg(NV - 1), :]
            beyond = jnp.where(sub == SUBS - 1, -pltpu.roll(inner, HALF, 1), wr[slot, w, at(1), :])
            fr[slot, w, reg(NV - 1), :] = cst * (inner + beyond)
        loop(NV, col_faces)

    def store(t):
        rows = [jnp.concatenate([st[0, i, w, nat(t), :] for i in range(slots)], axis=0) for w in range(NW)]
        line = lax.broadcasted_iota(I32, (slots * SUBS, LANES), 1)
        for top in PAIR:
            own_half = here.ftx + top * (1 - 2 * here.ftx)
            for part in PAIR:
                col = line + LANES * part
                col = (col + here.fty * (size - 1 - 2 * col) + OFF) & 255
                val = pick(col & 3, [lanes_of(v, HALF * own_half + (col >> 2)) for v in rows])
                first = pl.multiple_of(size + 68 - SUBS * t if top else SUBS * t, SUBS)
                for i in range(slots):
                    piece = val[SUBS * i:SUBS * i + SUBS]
                    tile_buf[0, i, part, at(first), :] = rev8(piece) if top else piece

    def clear(slot):
        def one(set_id):
            for qd in QUADS:
                rbuf_c[set_id, slot, qd] = jnp.zeros((SUBS, LANES), F32)
        loop(4, one)

    loop(slots, clear)
    vback[...] = jnp.zeros(vback.shape, F32)
    barrier = pltpu.get_barrier_semaphore()

    peers = 0
    for slot in range(slots):
        for qd in QUADS:
            for kind in range(3):
                device, _, _, _, stays = to(slot, qd, kind)

                @pl.when(jnp.logical_not(stays))
                def _():
                    pl.semaphore_signal(barrier, 1, device_id=device, device_id_type=MESH_ID)

                peers = peers + jnp.where(stays, 0, 1)

    def metric_in(v):
        for w in range(NW):
            corner = vertex & (lane < OFF // NW + 1) & (NW * lane + w < OFF) & (NV * sub + v < OFF)
            kk[w, reg(v), :] = jnp.where(corner, 0.0, k_in[w, reg(v), :])

    loop(NV, metric_in)
    load()
    pl.semaphore_wait(barrier, peers)

    def slot_of(i):
        if tiles * tiles * 2 != len(ORDER_OF) or slots != 3:
            return i
        at = (here.pd * tiles + here.tx) * tiles + here.ty
        code = jnp.int32(0)
        for name, order in ORDERS.items():
            value = sum(int(slot) << (2 * i) for i, slot in enumerate(order))
            for pos, other_name in enumerate(ORDER_OF):
                if other_name == name:
                    code = jnp.where(at == pos, value, code)
        return (code >> (2 * i)) & 3

    seven = (jnp.minimum(here.tx, 0) + 7).astype(F32)

    def one_round(turn_no):
        rnd = turn_no - 1

        def one_slot(slot):
            @pl.when(rnd >= 0)
            def _():
                def arrive(field):
                    set_id = jnp.where(field == 0, rnd & 1, field + 1)
                    wait_all(field, set_id, slot, False)
                    unpack(set_id, field, slot)

                loop(jnp.where(rnd == 0, 3, 1), arrive)

                @pl.when(rnd == 0)
                def _():
                    faces(slot)
                    vertex_setup(slot)

                def one_step(t):
                    for i in range(UNROLL):
                        s = ws[rnd * STEPS_PER_ROUND + UNROLL * t + i]
                        stage(xa, xb, xa, slot, s, seven, False)
                        stage(xb, xa, xa, slot, s, seven, True)

                loop(STEPS_PER_ROUND // UNROLL, one_step)
                loop(jnp.where(rnd == 0, 3, 1), lambda field: wait_all(field, 0, slot, True))

            @pl.when(rnd < rounds - 1)
            def _():
                def leave(field):
                    pack(field, slot)
                    send(field, jnp.where(field == 0, (rnd + 1) & 1, field + 1), slot)

                loop(jnp.where(rnd < 0, 3, 1), leave)

        loop(slots, lambda i: one_slot(slot_of(i)))

    loop(rounds + 1, one_round)
    loop(16, store, 4)
    loop(slots, rows_out)


def metric(tiles, size):
    cells = tiles * size
    step = 0.5 * math.pi / cells
    row = jnp.arange(LANES)
    row = 16 * (row % 8) + row // 8
    halves = jnp.arange(2)
    flip_x = lax.axis_index('tx') // (tiles // 2)
    flip_y = lax.axis_index('ty') // (tiles // 2)

    def square(pos, first):
        pos = pos + first * size
        pos = jnp.where(pos < 0, -1 - pos, pos)
        pos = jnp.where(pos >= cells, 2 * cells - 1 - pos, pos)
        tan = jnp.tan((pos.astype(F32) + 0.5) * step - 0.25 * math.pi)
        return tan * tan

    own = row[:, None] - OFF
    is_high = (halves[None, :] + flip_x) % 2
    sq_a = square(jnp.where(is_high == 1, size - 1 - own, own), lax.axis_index('tx'))
    sq_a = jnp.repeat(sq_a, HALF, axis=1)[None]
    col = 4 * jnp.arange(HALF)[None, :] + jnp.arange(NW)[:, None]
    own = col - OFF
    sq_b = square(jnp.where(flip_y == 1, size - 1 - own, own), lax.axis_index('ty'))
    sq_b = jnp.tile(sq_b, (1, 2))[:, None, :]
    r_sq = 1.0 + sq_a + sq_b
    val = (0.5 * C_SPEED * CFL_STEP) * (r_sq * jnp.sqrt(r_sq)) / ((1.0 + sq_a) * (1.0 + sq_b))
    first = OFF - HALO
    col = jnp.tile(col, (1, 2))[:, None, :]
    real = (row[None, :, None] >= first) & (col >= first) & (col < 4 * HALF - first)
    return jnp.where(real, val, 0.0)


def solution(mesh):
    tiles = mesh.shape['tx']
    slots = 6 // mesh.shape['panel']
    field_spec = P(('member', 'panel'), 'tx', 'ty')
    wind_spec = P('panel', 'tx', 'ty')

    def local_run(tracer, wind_a, wind_b, wind_scale):
        size = tracer.shape[1]
        steps = wind_scale.shape[0]
        vmem = pl.BlockSpec(memory_space=pltpu.VMEM)
        planes = pltpu.VMEM((slots, NW, LANES, LANES), F32)
        quad = (slots, 4)
        return pl.pallas_call(
            functools.partial(kernel, tiles, steps, size),
            out_shape=jax.ShapeDtypeStruct(tracer.shape, F32),
            in_specs=[pl.BlockSpec(memory_space=pltpu.SMEM)] + [vmem] * 4,
            out_specs=vmem,
            scratch_shapes=[
                pltpu.VMEM((3, slots, 2, size + OFF + 6, LANES), F32),
                pltpu.VMEM((3, slots, NW, LANES, LANES), F32), planes, planes, planes,
                pltpu.VMEM((slots, LANES, LANES), F32),
                pltpu.VMEM((NW, LANES, LANES), F32), pltpu.VMEM((NW, LANES, LANES), F32),
                pltpu.VMEM((NW + 1, LANES, LANES), F32),
                pltpu.VMEM((slots, NW, 4, 8, LANES), F32),
                pltpu.VMEM((2, NW, 32, LANES), F32), pltpu.VMEM((2, NW, 32, LANES), F32),
                pltpu.VMEM((4, LANES, LANES), F32), pltpu.VMEM((NW, LANES, LANES), F32),
                pltpu.VMEM((NW, HALF, LANES), F32),
                pltpu.VMEM((NW, LANES, LANES), F32),
                pltpu.VMEM((3, *quad, 2, 96, LANES), F32),
                pltpu.VMEM((3, *quad, 2, 8, LANES), F32),
                pltpu.VMEM((4, *quad, 2, HALO, LANES), F32),
                pltpu.VMEM((4, *quad, 8, LANES), F32),
                pltpu.SemaphoreType.DMA((3, *quad, 3)),
                pltpu.SemaphoreType.DMA((4, *quad, 3)),
            ],
            compiler_params=pltpu.CompilerParams(collective_id=0, has_side_effects=True, vmem_limit_bytes=60 * 2**20),
        )(wind_scale, tracer, wind_a, wind_b, metric(tiles, size))

    return jax.shard_map(local_run, mesh=mesh, in_specs=(field_spec, wind_spec, wind_spec, P()),
                         out_specs=field_spec, check_vma=False)
```

time: 196 us -> 169 us (0.86)
  Pallas kernels: 187 us -> 166 us
  local copies, waits for them, and re-layouts: 4.96 us -> 2.27 us
    pallas_call x1, Pallas kernels: 187 us -> 166 us  [local_run(): pl.pallas_call(functools.partial(kernel, tiles, steps, size), out_shape=j...]
where the time goes in v2:
time: 169 us
  Pallas kernels  166 us (98%)
  local copies, waits for them, and re-layouts  2.27 us (1%)
    pallas_call x1, Pallas kernels, local_run(): pl.pallas_call(functools.partial(kernel, tiles, steps, size), out_shape=j...  166 us

profile of v2, /device:TPU:97, one launch (start us, length us, event | category | flops | bytes accessed | tf_op | source)
XLA Modules:
  0.0 169.1 jit_solution(9869865223029765250)
XLA Ops:
  0.0 0.1 fusion.9
  0.1 0.1 fusion.18
  0.3 0.1 ge.46
  0.4 0.1 lt.50
  0.4 0.1 tile.19
  0.5 0.1 copy.5
  0.6 0.9 fusion.2.k_in
  1.5 165.7 %shard_map.46 = f32[3,180,180]{2,1,0:T(8,128)} custom-call(f32[64]{0:T(128)} %ws.1, f32[3,180,180]{2,1,0:T(8,128)} %q_in.1, f32[3,180,180]{2,1,0:T(8,128)} %wa_in.1, f32[3,180,180]{2,1,0:T(8,128)} %wb_in.1, f32[4,128,128]{2,1,0:T(8,128)} %fusion.2.k_in), custom_call_target="tpu_custom_call" | custom-call | tf_op jit(solution)/shard_map/pallas_call | solution.py:617
  167.2 1.9 %copy.7 = f32[3,180,180]{2,1,0:T(8,128)} copy(f32[3,180,180]{2,1,0:T(8,128)} %shard_map.46) | data formatting | bytes 777600
  (10 shorter events, 0.1 us)

commit v3 on v2

--- a/solution.py
+++ b/solution.py
@@ -18,7 +18,8 @@
 OFF = 38
 HALO = 32
 STEPS_PER_ROUND = 8
-NIBBLE = 4
+PLACE = 12
+STAYS = 20
 SUBS = 8
 VROW = 49
 HALF = 64
@@ -29,7 +30,6 @@
 ORDER_OF = 'abbbaaaacccccccc' + 'bacdbacdbacdaacd'
 F32 = jnp.float32
 I32 = jnp.int32
-MESH_ID = pl.DeviceIdType.MESH
 
 
 def lane_id():
@@ -73,6 +73,7 @@
     def __init__(self, tiles, panels_per_dev):
         self.n, self.lp = tiles, panels_per_dev
         self.tx, self.ty, self.pd = lax.axis_index('tx'), lax.axis_index('ty'), lax.axis_index('panel')
+        self.member, self.panel_devs = lax.axis_index('member'), 6 // panels_per_dev
         self.ftx, self.fty = self.flip(self.tx), self.flip(self.ty)
         self.edge_x = self.at_edge(self.tx)
         self.edge_y = self.at_edge(self.ty)
@@ -150,79 +151,67 @@
 
     def plan(slot, qd, kind):
         h, k = qd >> 1, qd & 1
-        dest = here.corner(slot, h, k) if kind == 2 else here.face(slot, h, k, kind)
-        code = dest[0]
-        for i, part in enumerate((dest[1], dest[2], dest[3], 2 * dest[4] + dest[5], dest[6])):
-            code = code + (part << (NIBBLE * (i + 1)))
-        if kind == 2:
-            if qd:
-                return code
-            stays = vertex
-        elif (h, k)[kind]:
+        pd, slot2, tx, ty, h2, k2, kind2 = here.corner(slot, h, k) if kind == 2 else here.face(slot, h, k, kind)
+        place = SUBS * slot2 + 4 * h2 + 2 * k2 + kind2
+        code = ((here.member * tiles + ty) * tiles + tx) * here.panel_devs + pd + (place << PLACE)
+        if not may_stay(qd, kind):
             return code
-        else:
-            stays = (dest[0] == here.pd) & (dest[2] == here.tx) & (dest[3] == here.ty)
-        return code + jnp.where(stays, 1 << (6 * NIBBLE), 0)
+        stays = vertex if kind == 2 else (pd == here.pd) & (tx == here.tx) & (ty == here.ty)
+        return code + jnp.where(stays, 1 << STAYS, 0)
+
+    def may_stay(qd, kind):
+        return qd == 0 if kind == 2 else (qd >> 1, qd & 1)[kind] == 0
 
     plans = [[[plan(slot, qd, kind) for kind in range(3)] for qd in QUADS] for slot in range(slots)]
 
-    def code_of(slot, qd, kind):
-        return pick(slot, [plans[i][qd][kind] for i in range(slots)])
-
     def to(slot, qd, kind):
-        code = code_of(slot, qd, kind)
-        pd, slot2, tx, ty, qd2, kind2 = [(code >> (NIBBLE * i)) & ((1 << NIBBLE) - 1) for i in range(6)]
-        return {'panel': pd, 'tx': tx, 'ty': ty}, slot2, qd2, kind2, (code >> (6 * NIBBLE)) == 1
-
-    def leaves(slot, qd, kind):
-        return (code_of(slot, qd, kind) >> (6 * NIBBLE)) == 0
+        code = pick(slot, [plans[i][qd][kind] for i in range(slots)])
+        return code & ((1 << PLACE) - 1), (code >> PLACE) & ((1 << (STAYS - PLACE)) - 1), code >= 1 << STAYS
 
     def send(field, set_id, slot):
         for qd in QUADS:
             for kind in range(3):
-                device, slot2, qd2, kind2, stays = to(slot, qd, kind)
+                device, place, stays = to(slot, qd, kind)
+                slot2 = place >> 3
                 if kind < 2:
-                    src, dst = strip.at[field, slot, qd, kind, pl.ds(SUBS, HALO)], rbuf.at[set_id, slot2, qd2, kind2]
-                    sem = recv_sem.at[set_id, slot2, qd2, kind2]
+                    src, dst = strip.at[field, slot, qd, kind, pl.ds(SUBS, HALO)], rbuf.at[set_id, place]
                 else:
-                    src, dst = strip_c.at[field, slot, qd, kind2], rbuf_c.at[set_id, slot2, qd2]
-                    sem = recv_sem.at[set_id, slot2, qd2, 2]
-
-                @pl.when(jnp.logical_not(stays))
-                def _():
+                    src, dst = strip_c.at[field, slot, qd, place & 1], rbuf_c.at[set_id, place >> 1]
+
+                def start():
                     pltpu.make_async_remote_copy(
-                        src_ref=src, dst_ref=dst, send_sem=send_sem.at[field, slot, qd, kind], recv_sem=sem,
-                        device_id=device, device_id_type=MESH_ID).start()
-
-                if kind < 2 and (qd >> 1, qd & 1)[kind] == 0:
+                        src_ref=src, dst_ref=dst, send_sem=send_sem.at[field, slot, kind // 2],
+                        recv_sem=recv_sem.at[set_id, slot2, kind // 2],
+                        device_id=device, device_id_type=pl.DeviceIdType.LOGICAL).start()
+
+                if not may_stay(qd, kind):
+                    start()
+                    continue
+                pl.when(jnp.logical_not(stays))(start)
+                if kind < 2:
                     @pl.when(stays)
                     def _():
                         for g in QUADS:
-                            rbuf[set_id, slot2, qd2, kind2, reg(g), :] = (
-                                strip[field, slot, qd, kind, at(8 + SUBS * g), :])
+                            rbuf[set_id, place, reg(g), :] = strip[field, slot, qd, kind, at(SUBS + SUBS * g), :]
 
     def wait_all(field, set_id, slot, sent):
-        for qd in QUADS:
-            for kind in range(3):
-                if kind < 2:
-                    src, dst = strip.at[field, slot, qd, kind, pl.ds(SUBS, HALO)], rbuf.at[set_id, slot, qd, kind]
-                else:
-                    src, dst = strip_c.at[field, slot, qd, 0], rbuf_c.at[set_id, slot, qd]
-
-                def wait():
-                    copy = pltpu.make_async_remote_copy(
-                        src_ref=src, dst_ref=dst, send_sem=send_sem.at[field, slot, qd, kind],
-                        recv_sem=recv_sem.at[set_id, slot, qd, kind],
-                        device_id={'panel': here.pd, 'tx': here.tx, 'ty': here.ty}, device_id_type=MESH_ID)
-                    if sent:
-                        copy.wait_send()
-                    else:
-                        copy.wait_recv()
-
-                if (qd == 0) if kind == 2 else ((qd >> 1, qd & 1)[kind] == 0):
-                    pl.when(leaves(slot, qd, kind))(wait)
-                else:
-                    wait()
+        def wait(kind, count):
+            ref = rbuf.at[set_id, pl.ds(SUBS * slot, count)] if kind == 0 else rbuf_c.at[set_id, pl.ds(4 * slot, count)]
+            copy = pltpu.make_async_remote_copy(
+                src_ref=ref, dst_ref=ref, send_sem=send_sem.at[field, slot, kind], recv_sem=recv_sem.at[set_id, slot, kind],
+                device_id=to(slot, 3, 0)[0], device_id_type=pl.DeviceIdType.LOGICAL)
+            if sent:
+                copy.wait_send()
+            else:
+                copy.wait_recv()
+
+        some_stay = jnp.int32(0)
+        for qd, kind in ((0, 0), (1, 0), (0, 1), (2, 1)):
+            some_stay = some_stay + to(slot, qd, kind)[2].astype(I32)
+        for stay in range(3):
+            pl.when(some_stay == stay)(functools.partial(wait, 0, SUBS - stay))
+        pl.when(vertex)(lambda: wait(1, 3))
+        pl.when(jnp.logical_not(vertex))(lambda: wait(1, 4))
 
     def other(field):
         return jnp.where(field == 0, 0, 3 - field)
@@ -264,8 +253,8 @@
         for qd in QUADS:
             parts = []
             for g in reversed(QUADS):
-                face = rbuf[set_id, slot, qd, 0, reg(g), :] * row_sign[qd & 1]
-                block = pltpu.roll(rbuf_c[set_id, slot, qd], (6 - 32 * g) % LANES, 1) * block_sign[qd & 1]
+                face = rbuf[set_id, SUBS * slot + 2 * qd, reg(g), :] * row_sign[qd & 1]
+                block = pltpu.roll(rbuf_c[set_id, 4 * slot + qd], (6 - 32 * g) % LANES, 1) * block_sign[qd & 1]
                 parts.append(rev8(jnp.where(lane < OFF, block, face)))
             vals.append(jnp.concatenate(parts, axis=0))
         for w in range(NW):
@@ -284,9 +273,9 @@
             low = 1 if w >= 2 else 2
             for h in PAIR:
                 turn[w, at(HALF * h + low), :] = rev8(
-                    rbuf[set_id, slot, 2 * h, 1, pl.ds((1, 0, 3, 2)[w], 8, stride=4), :])
+                    rbuf.at[set_id, SUBS * slot + 4 * h + 1][pl.ds((1, 0, 3, 2)[w], 8, stride=4), :])
                 turn[w, at(HALF * h + 53 + low), :] = (
-                    rbuf[set_id, slot, 2 * h + 1, 1, pl.ds((2, 3, 0, 1)[w], 8, stride=4), :])
+                    rbuf.at[set_id, SUBS * slot + 4 * h + 3][pl.ds((2, 3, 0, 1)[w], 8, stride=4), :])
             turned = turn[w].T
             inside = ((lb >= low) & (lb < low + 8)) | ((lb >= 53 + low) & (lb < 61 + low))
             first = inside & (sub >= 6)
@@ -486,7 +475,7 @@
     def clear(slot):
         def one(set_id):
             for qd in QUADS:
-                rbuf_c[set_id, slot, qd] = jnp.zeros((SUBS, LANES), F32)
+                rbuf_c[set_id, 4 * slot + qd] = jnp.zeros((SUBS, LANES), F32)
         loop(4, one)
 
     loop(slots, clear)
@@ -494,16 +483,25 @@
     barrier = pltpu.get_barrier_semaphore()
 
     peers = 0
-    for slot in range(slots):
-        for qd in QUADS:
-            for kind in range(3):
-                device, _, _, _, stays = to(slot, qd, kind)
-
-                @pl.when(jnp.logical_not(stays))
-                def _():
-                    pl.semaphore_signal(barrier, 1, device_id=device, device_id_type=MESH_ID)
-
-                peers = peers + jnp.where(stays, 0, 1)
+    for qd, kind in ((0, 0), (2, 0), (0, 1), (1, 1), (0, 2), (1, 2), (2, 2), (3, 2)):
+        crosses = 0
+        if kind != 1 and qd < 2:
+            crosses = here.edge_x
+        if kind != 0 and not qd & 1:
+            crosses = crosses | here.edge_y
+        for slot in range(slots):
+            device, _, stays = to(slot, qd, kind)
+            greets = jnp.logical_not(stays)
+            if slot:
+                if isinstance(crosses, int):
+                    continue
+                greets = greets & (crosses == 1)
+
+            @pl.when(greets)
+            def _():
+                pl.semaphore_signal(barrier, 1, device_id=device, device_id_type=pl.DeviceIdType.LOGICAL)
+
+            peers = peers + jnp.where(greets, 1, 0)
 
     def metric_in(v):
         for w in range(NW):
@@ -632,10 +630,10 @@
                 pltpu.VMEM((NW, LANES, LANES), F32),
                 pltpu.VMEM((3, *quad, 2, 96, LANES), F32),
                 pltpu.VMEM((3, *quad, 2, 8, LANES), F32),
-                pltpu.VMEM((4, *quad, 2, HALO, LANES), F32),
-                pltpu.VMEM((4, *quad, 8, LANES), F32),
-                pltpu.SemaphoreType.DMA((3, *quad, 3)),
-                pltpu.SemaphoreType.DMA((4, *quad, 3)),
+                pltpu.VMEM((4, SUBS * slots, HALO, LANES), F32),
+                pltpu.VMEM((4, 4 * slots, 8, LANES), F32),
+                pltpu.SemaphoreType.DMA((3, slots, 2)),
+                pltpu.SemaphoreType.DMA((4, slots, 2)),
             ],
             compiler_params=pltpu.CompilerParams(collective_id=0, has_side_effects=True, vmem_limit_bytes=60 * 2**20),
         )(wind_scale, tracer, wind_a, wind_b, metric(tiles, size))

time: 169 us -> 164 us (0.970)
  Pallas kernels: 166 us -> 161 us
    pallas_call x1, Pallas kernels: 166 us -> 161 us  [local_run(): pl.pallas_call(functools.partial(kernel, tiles, steps, size), out_shape=j...]
where the time goes in v3:
time: 164 us
  Pallas kernels  161 us (98%)
  local copies, waits for them, and re-layouts  2.27 us (1%)
    pallas_call x1, Pallas kernels, local_run(): pl.pallas_call(functools.partial(kernel, tiles, steps, size), out_shape=j...  161 us

profile of v3, /device:TPU:97, one launch (start us, length us, event | category | flops | bytes accessed | tf_op | source)
XLA Modules:
  0.0 164.1 jit_solution(14045223898002728333)
XLA Ops:
  0.0 0.1 fusion.9
  0.1 0.1 fusion.18
  0.3 0.1 ge.46
  0.4 0.1 lt.50
  0.4 0.1 tile.19
  0.5 0.1 copy.5
  0.6 0.9 fusion.2.k_in
  1.5 160.7 %shard_map.46 = f32[3,180,180]{2,1,0:T(8,128)} custom-call(f32[64]{0:T(128)} %ws.1, f32[3,180,180]{2,1,0:T(8,128)} %q_in.1, f32[3,180,180]{2,1,0:T(8,128)} %wa_in.1, f32[3,180,180]{2,1,0:T(8,128)} %wb_in.1, f32[4,128,128]{2,1,0:T(8,128)} %fusion.2.k_in), custom_call_target="tpu_custom_call" | custom-call | tf_op jit(solution)/shard_map/pallas_call | solution.py:615
  162.2 1.9 %copy.7 = f32[3,180,180]{2,1,0:T(8,128)} copy(f32[3,180,180]{2,1,0:T(8,128)} %shard_map.46) | data formatting | bytes 777600
  (10 shorter events, 0.1 us)
